TPU v7x, 128 devices: a whole 4x4x4 slice. The times are simulated.
128 devices in a mesh: datb: 4 (over z), model: 4 (over y), data: 8 (over x, core).
Axes of the slice: x: 4, y: 4, z: 4, core: 2. Of those that a mesh axis runs over, the one named last changes fastest.
Arguments:
- tokens: bfloat16 [8192, 3584], P(('datb', 'data', 'model'))
- w_gate: bfloat16 [3584, 18944], P(('datb', 'data'), 'model')
- w_up: bfloat16 [3584, 18944], P(('datb', 'data'), 'model')
- w_down: bfloat16 [18944, 3584], P('model', ('datb', 'data'))
- grad_out: bfloat16 [8192, 3584], P(('datb', 'data', 'model'))
Outputs:
- output 1: bfloat16 [8192, 3584], P(('datb', 'data', 'model'))
- output 2: bfloat16 [8192, 3584], P(('datb', 'data', 'model'))
- output 3: float32 [3584, 18944], P(('datb', 'data'), 'model')
- output 4: float32 [3584, 18944], P(('datb', 'data'), 'model')
- output 5: float32 [18944, 3584], P('model', ('datb', 'data'))
All inputs are finite; a program needn't handle non-finite values.
Results may differ from a plain program's by a relative error of at most 0.02.
Values are sent between devices in bfloat16 or wider.
A program may use at most 1 GiB of HBM per device.

v0:
```python
import functools

import jax
import jax.numpy as jnp
from jax import lax
from jax.experimental import pallas as pl
from jax.experimental.pallas import tpu as pltpu
from jax.sharding import Mesh
from jax.sharding import PartitionSpec as P

ROW_SPEC = P(("datb", "x", "core", "model"), None)
GATE_SPEC = P(("datb", "x", "core"), "model")
DOWN_SPEC = P("model", ("datb", "x", "core"))
BF16 = jnp.bfloat16
F32 = jnp.float32
MESH_ID = pl.DeviceIdType.MESH
RING = 4
NEAR = ((0, 0), (0, 1), (1, 0), (3, 0), (1, 1), (3, 1), (2, 0), (2, 1))
DELTAS = (0, 3, 1, 2)
LANE = 128
OUT_COLS = 512
EX, Z1, Z2, P1, P2, BL, Q1, Q2, WD, CI = range(10)
GATHER_STEPS = (
    (Z1, 0, 0), (P1, 0, 0), (P1, 0, 1), (EX, 0, 1), (BL, 0, 0), (P1, 2, 0), (P1, 2, 1), (EX, 0, 2), (Z1, 3, 0), (EX, 3, 1), (EX, 3, 2),
    (EX, 3, 3), (EX, 3, 4), (EX, 3, 5), (EX, 3, 6), (EX, 3, 7), (Z1, 1, 0), (EX, 1, 1), (Z1, 2, 0), (EX, 2, 1), (EX, 0, 3), (BL, 1, 0),
    (Z1, 3, 1), (EX, 0, 4), (EX, 0, 5), (Z1, 0, 1), (Z1, 1, 1), (Z2, 3, 0, 0), (Z1, 2, 1), (EX, 0, 6), (EX, 0, 7), (Z2, 0, 0, 0),
    (Z2, 1, 0, 0), (EX, 1, 2), (EX, 1, 3), (Z2, 2, 0, 0), (Z2, 3, 0, 1), (P2, 0, 0), (P2, 0, 1), (BL, 0, 1), (Q1, 0, 0, 1), (Z1, 3, 2),
    (Z1, 3, 3), (Z1, 3, 4), (Q1, 0, 0, 0), (Z1, 3, 5), (Z2, 0, 0, 1), (EX, 1, 4), (EX, 1, 5), (P2, 2, 1), (Z1, 3, 6), (EX, 1, 6),
    (EX, 1, 7), (Z1, 3, 7), (Z1, 0, 2), (Q1, 1, 0, 1), (Z2, 3, 1, 0), (Z2, 3, 1, 1), (Z1, 0, 3), (EX, 2, 2), (EX, 2, 3), (Z2, 3, 1, 2),
    (BL, 0, 2), (Z2, 3, 1, 3), (Z1, 0, 4), (EX, 2, 4), (EX, 2, 5), (Z1, 0, 5), (EX, 2, 6), (EX, 2, 7), (Z2, 3, 0, 2), (Q1, 0, 1, 1),
    (Z2, 3, 0, 3), (Z1, 0, 6), (P1, 1, 0), (P1, 1, 1), (Q1, 0, 1, 0), (Z1, 0, 7), (BL, 2, 2), (Z2, 0, 1, 0), (Z1, 1, 2), (Z2, 0, 1, 1),
    (Z2, 0, 0, 2), (Q2, 0, 0), (Z2, 0, 1, 2), (Z2, 0, 0, 3), (BL, 2, 0), (BL, 0, 3), (Q1, 0, 2, 1), (Z2, 0, 1, 3), (Z1, 1, 3), (Z1, 1, 4),
    (WD, 3), (Z1, 1, 5), (Q1, 0, 2, 0), (Z1, 1, 6), (P2, 2, 0), (BL, 2, 1), (P2, 1, 0), (P2, 1, 1), (Z1, 1, 7), (Q1, 0, 3, 1),
    (Q1, 1, 0, 0), (Z2, 1, 0, 1), (Q1, 2, 2, 0), (Q1, 2, 2, 1), (Z2, 1, 0, 2), (BL, 1, 1), (Q2, 0, 1), (WD, 0), (Z2, 1, 1, 0), (CI, 0),
)
GATE_STEPS = (
    (),
    (),
    (
        (Z1, 2, 2),
    ),
    (
        (Q2, 0, 2), (Z2, 1, 1, 1), (Z2, 1, 0, 3), (Q1, 2, 0, 0), (Q1, 2, 0, 1), (BL, 1, 2), (CI, 1),
    ),
    (
        (Z2, 1, 1, 2), (Z1, 2, 3),
    ),
    (
        (Q1, 0, 3, 0), (Z2, 1, 1, 3), (Z1, 2, 4), (CI, 2),
    ),
    (
        (Z1, 2, 5), (Q1, 2, 1, 0), (Q1, 2, 1, 1), (BL, 2, 3), (BL, 1, 3), (Z1, 2, 6), (Q2, 0, 3),
    ),
    (
        (Q2, 1, 0), (Z1, 2, 7), (CI, 3),
    ),
    (
        (Q2, 2, 0), (Q2, 2, 2), (Z2, 2, 0, 1), (Q1, 1, 1, 0), (Q1, 1, 1, 1),
    ),
)
UP_STEPS = (
    (
        (Z2, 2, 0, 2), (Q1, 1, 2, 1), (WD, 1),
    ),
    (
        (Q2, 2, 1), (Q1, 2, 3, 1), (Q1, 1, 2, 0),
    ),
    (
        (Z2, 2, 1, 0), (Z2, 2, 0, 3), (Q1, 1, 3, 1),
    ),
    (
        (Z2, 2, 1, 1), (Q1, 1, 3, 0),
    ),
    (
        (Q2, 1, 2), (Z2, 2, 1, 2), (Q1, 2, 3, 0),
    ),
    (
        (Q2, 1, 1), (Z2, 2, 1, 3),
    ),
    (
        (Q2, 1, 3), (Q2, 2, 3),
    ),
    (),
)
LATE_STEPS = (
    (WD, 2),
)
Z_ORDER = (2, 0, 1)
EARLY_ORDER = (
    ("far_block", 2), ("next_products", 2), ("late",), ("give_rows", 0),
)
LATE_ORDER = (
    ("next_adds", 2), ("own_block", 2), ("keep_rows", 0), ("ring_first", 0, 1), ("finish", 2, 0), ("far_block", 0), ("give_rows", 1),
    ("finish", 2, 3), ("finish", 2, 1), ("finish", 2, 4), ("ring_dependent", 0, 1), ("finish", 2, 2), ("far_block", 1), ("keep_rows", 1),
    ("ring_first", 1, 1), ("next_blocks", 0), ("own_block", 0), ("next_blocks", 1), ("own_block", 1), ("finish", 0, 0),
    ("ring_dependent", 1, 1), ("finish", 0, 1), ("ring_last", 0, 1), ("ring_first", 0, 2), ("finish", 0, 2), ("finish", 0, 3),
    ("finish", 0, 4), ("ring_last", 1, 1), ("ring_first", 1, 2), ("ring_dependent", 0, 2), ("finish", 1, 0), ("ring_dependent", 1, 2),
    ("ring_last", 0, 2), ("finish", 1, 1), ("finish", 1, 2), ("ring_last", 1, 2), ("finish", 1, 3), ("finish", 1, 4),
)


def dot(a, b, ca, cb):
    return lax.dot_general(a, b, (((ca,), (cb,)), ((), ())), preferred_element_type=F32)


def layer_kernel(sg, su, sd, tok, grad, tok_own, grad_own,
                 og, ou, od, out, gin, wg, wu, wd, wr, tok_all, grad_all, h_main, h_rest, ra, rb, give, rc, part, ra1, rb1, sd1, mid, ra2, rb2, sd2,
                 ff, blk, far, nxt,
                 own_sem, ex_s, ex_r, z1_s, z1_r, zn_r, z2_s, p1_s, p1_r, p2_s, p2_r, q1_s, q1_r, q2_s, q2_r, cc_s, cc_r,
                 sh_sem, wv_sem, row_sem, hst_sem, blk_sem, tmp_sem, a_s, a_r, u_s, u_r, e_s, e_r, out_sem,
                 c_s, c_r, a1_s, a1_r, f1_s, f1_r, a2_s, a2_r, f2_s, f2_r):
    z, y = lax.axis_index("datb"), lax.axis_index("model")
    x, core = lax.axis_index("x"), lax.axis_index("core")
    i8 = 2 * x + core
    n8 = 2 * RING
    rows, d = tok.shape
    half_rows = rows // 2
    chunk = RING * rows
    n_chunk = n8
    nf, tokens = ff.shape[1:]
    dp = sg.shape[0]
    half = nf // 2
    main = wg.shape[1]
    rest = nf - main
    packed = wr.shape[1]
    cols = blk.shape[2]
    tiles = far.shape[1] // LANE
    outs = (og, ou, od)

    zs, ys, xs = ([v] + [lax.rem(v + k, RING) for k in range(1, RING)] for v in (z, y, x))
    cores = (core, 1 - core)
    peers = [[2 * v + c for c in cores] for v in xs]
    slot_at = [[[pl.multiple_of((zz * n8 + peers[dx][dc]) * dp, 16) for dc in range(2)] for dx in range(RING)] for zz in zs]
    hand_at = [[pl.multiple_of(p * dp, 8) for p in row] for row in peers]
    rows_at = [[[pl.multiple_of((peers[dx][dc] * RING + yy) * rows, half_rows) for dc in range(2)] for yy in ys] for dx in range(RING)]
    lanes_at = [pl.multiple_of(zz * cols, LANE) for zz in zs]

    def peer(dx, dc):
        return peers[dx][dc]

    def zdev(k):
        return {"datb": zs[k]}

    def xdev(k):
        return {"x": xs[k]}

    def ydev(k):
        return {"model": ys[k]}

    def near(dx, dc):
        return {"x": xs[dx], "core": cores[dc]}

    def copy(src, dst, s, r, dev):
        return pltpu.make_async_remote_copy(src_ref=src, dst_ref=dst, send_sem=s, recv_sem=r, device_id=dev, device_id_type=MESH_ID)

    rcopy = copy

    def all_in(ref, sem):
        copy(ref, ref, sem, sem, zdev(1)).wait_recv()

    def all_out(ref, sem):
        copy(ref, ref, sem, sem, zdev(1)).wait_send()

    def start(copies):
        for c in copies:
            c.start()

    def received(copies):
        for c in copies:
            c.wait_recv()

    def sent(copies):
        for c in copies:
            c.wait_send()

    def run_order(fns, order):
        for fn, *args in order:
            with jax.named_scope("_".join(str(v) for v in [fn, *args])):
                fns[fn](*args)

    barrier = pltpu.get_barrier_semaphore()
    others = [zdev(1), zdev(3), ydev(1), ydev(3)] + [near(*n) for n in NEAR[1:]]
    for dev in others:
        pl.semaphore_signal(barrier, inc=1, device_id=dev, device_id_type=MESH_ID)

    def blk_load(t, slot, k):
        src = tok_all if t < 2 else grad_all
        return pltpu.make_async_copy(src.at[:, pl.ds(lanes_at[k], cols)], blk.at[slot], blk_sem.at[slot])

    plan = []
    for fn, *args in EARLY_ORDER + LATE_ORDER:
        plan += [(args[0], k) for k in {"far_block": (2,), "next_blocks": (1, 3), "next_products": (1, 3), "own_block": (0,)}.get(fn, ())]
    taken = []

    def next_block():
        n = len(taken)
        taken.append(n)
        blk_load(plan[n][0], n % 2, plan[n][1]).wait()
        if n + 1 < len(plan):
            blk_load(plan[n + 1][0], (n + 1) % 2, plan[n + 1][1]).start()
        return n % 2

    def product(t, dst, then=None):
        slot = next_block()
        step = 2 * LANE
        count = -(-cols // step)

        def one(n, carry):
            lanes = pl.ds(pl.multiple_of(jnp.minimum(n * step, cols - step), LANE), step)
            dst[:nf, lanes] = jnp.dot(ff[t], blk[slot, :, lanes], preferred_element_type=F32)
            for k in range(count if then else 0):
                first = k * step if k < count - 1 else cols - step
                size = step if k == count - 1 else min(step, cols - step - first)
                if size > 0:
                    pl.when(n == k)(functools.partial(then, first, size))
            return carry

        lax.fori_loop(0, count, one, 0)

    lo, hi = pl.ds(0, half), pl.ds(half, half)

    def a_copies(t, first=0, size=cols):
        lanes = pl.ds(first, size)
        return [rcopy(far.at[t, at, lanes], ra.at[t, at, lanes], a_s.at[t], a_r.at[t], zdev(k)) for at, k in ((lo, 1), (hi, 3))]

    def tile_rows(tile):
        return pl.ds(tile * LANE, min(LANE, nf - tile * LANE))

    def unit_parts(t, tile):
        if (t, tile) != (Z_ORDER[2], tiles - 1):
            return [(tile, 0, cols)]
        first = -(-cols // 2 // LANE) * LANE
        return [(tile, 0, first), (tiles, first, cols - first)]

    def unit_copies(t, tile):
        at = tile_rows(tile)
        cs = []
        for n, first, size in unit_parts(t, tile):
            lanes = pl.ds(first, size)
            cs += [rcopy(nxt.at[t, s, at, lanes], rb.at[t, s, at, lanes], u_s.at[t], u_r.at[t, n], zdev(1 + 2 * s)) for s in range(2)]
        return cs

    def far_block(t):
        if t == Z_ORDER[0]:
            product(t, far.at[t], lambda first, size: start(a_copies(t, first, size)))
        else:
            product(t, far.at[t])
            start(a_copies(t))

    def early_units(t):
        if ("next_products", t) not in EARLY_ORDER + LATE_ORDER:
            return ()
        free = [(0, tile) for tile in range(tiles) if tile * LANE >= half]
        return free + [(1, tile) for tile in range(tiles) if (tile + 1) * LANE <= half]

    def next_products(t):
        for s in range(2):
            product(t, nxt.at[t, s])
        for s, tile in early_units(t):
            unit_copies(t, tile)[s].start()

    blocks = d // min(OUT_COLS, d)
    width = d // blocks

    def row_products(r, keep):
        side = core if keep else 1 - core
        specs, args = [], []
        for h, j, w in ((h_main, 2, wd), (h_rest, 0, wr)) if r == 0 else ((h_main, 0, wg), (h_main, 1, wu), (h_rest, 1, wr)):
            n = w.shape[1]
            specs += [pl.BlockSpec((1, RING, 1, RING * rows, n), lambda i, j=j: (j, 0, side, 0, 0)), pl.BlockSpec((width, n), lambda i: (i, 0))]
            args += [h, w]
        wide = pl.BlockSpec((RING, RING, rows, width), lambda i: (0, 0, 0, i))
        terms = len(args) // 2
        if keep:
            specs.append(wide)
            args.append(rc.at[r])

        def body(*refs):
            total = None
            for i in range(terms):
                h = refs[2 * i][...].reshape(RING * RING * rows, refs[2 * i].shape[-1])
                prod = dot(h, refs[2 * i + 1][...], 1, 1)
                total = prod if total is None else total + prod
            if keep:
                total = total + refs[-2][...].astype(F32).reshape(total.shape)
            refs[-1][...] = total.astype(BF16).reshape(RING, RING, rows, width)

        pltpu.emit_pipeline(body, grid=(blocks,), in_specs=specs, out_specs=[wide])(*args, (part if keep else give).at[r])

    def core_copy(r):
        return rcopy(give.at[r], rc.at[r], c_s.at[r], c_r.at[r], near(0, 1))

    def give_rows(r):
        row_products(r, False)
        core_copy(r).start()

    def forward_phase(rowbuf, av, bv, gv, hst, hst_rest, wv_a, wv_r):
        held = {}

        fulls = (wg, wu, wd, wr)
        REST = 3
        def shard_load(t):
            return pltpu.make_async_copy((sg, su, sd)[t], held["shard"].at[t], sh_sem.at[t])

        def cut_pieces(t):
            if t == REST:
                for u in range(3):
                    for j in range(n8):
                        held["rests"][j, :, u * rest:(u + 1) * rest] = held["shard"][u, :, j * nf + main:(j + 1) * nf]
            else:
                for j in range(n8):
                    held["pieces"][t, j] = held["shard"][t, :, j * nf:j * nf + main]
            own_piece(t).start()

        def piece(t, j):
            return held["rests"].at[j] if t == REST else held["pieces"].at[t, j]

        def own_piece(t):
            return pltpu.make_async_copy(piece(t, i8), slot(t, 0, NEAR[0]), own_sem.at[t])

        def go(make, *args):
            make(*args).start()

        def slot(t, k, source):
            dx, dc = source
            return fulls[t].at[pl.ds(slot_at[k][dx][dc], dp)]

        def source(k):
            dx, dc = NEAR[k]
            return (RING - dx) % RING, dc

        def back(side):
            return 3 if side == 0 else 1

        def ahead(side):
            return 1 if side == 0 else 3

        def exchange_copy(t, k):
            return copy(piece(t, peer(*NEAR[k])), slot(t, 0, NEAR[0]), ex_s.at[t], ex_r.at[t, k], near(*NEAR[k]))

        def exchange(t, k):
            go(exchange_copy, t, k)

        def z_first_copy(t, side, k):
            here = slot(t, 0, source(k))
            return copy(here if k else piece(t, i8), here, z1_s.at[t], z1_sem(t, side, k), zdev(ahead(side)))

        def z_first(t, k):
            if k:
                here = slot(t, 0, source(k))
                all_in(here, ex_r.at[t, k])
            for side in range(2):
                go(z_first_copy, t, side, k)

        def z1_sem(t, side, k):
            return z1_r.at[t, side, k % (n8 // 2)] if (k < n8 // 2) == (side == 0) else zn_r.at[t]

        def some(t, count):
            return fulls[t].at[pl.ds(0, count * dp)]

        def z_second_copy(t, side, k):
            there = slot(t, back(side), source(k + side * (n8 // 2)))
            return copy(there, there, z2_s.at[t], zn_r.at[t], zdev(ahead(side)))

        def z_second(t, side, k):
            kk = k + side * (n8 // 2)
            all_in(slot(t, back(side), source(kk)), z1_sem(t, side, kk))
            go(z_second_copy, t, side, k)

        def weights_done(t):
            if (WD, t) not in LATE_STEPS:
                own_wait(t)
            all_in(some(t, 2 * n8), zn_r.at[t])
            w_load(t).start()

        cut = d * 11 // 28
        rings = ((tok, tok_all, pl.ds(0, d), True), (grad, grad_all, pl.ds(0, cut), True), (grad, grad_all, pl.ds(cut, d - cut), False))

        def axis(r, n):
            return xdev if rings[r][3] == (n == 1) else ydev

        def block(r, da, db, flip=0, lo=0, size=rows):
            dx, dy = (da, db) if rings[r][3] else (db, da)
            first = rows_at[dx][dy][flip]
            return rings[r][1].at[pl.ds(pl.multiple_of(first + lo, half_rows) if lo else first, size), rings[r][2]]

        def own_block(r):
            return rings[r][0].at[:, rings[r][2]]

        def to_core_copy(r, ia, ib):
            there = block(r, DELTAS[ia], DELTAS[ib])
            return copy(own_block(r) if ia == 0 and ib == 0 else there, there, cc_s.at[r], cc_r.at[ia if r == 0 else RING - 1 + r], near(0, 1))

        def to_core(r, ia, ib):
            go(to_core_copy, r, ia, ib)

        def first_copy(r, side):
            return copy(own_block(r), block(r, 0, 0), p1_s.at[r], p1_r.at[r, side], axis(r, 1)(ahead(side)))

        def first_own(r, side):
            go(first_copy, r, side)

        def first_far_copy(r, side):
            part = block(r, back(side), 0, 0, side * half_rows, half_rows)
            return copy(part, part, p2_s.at[r], p2_r.at[r], axis(r, 1)(ahead(side)))

        def first_forward(r, side):
            there = block(r, back(side), 0)
            all_in(there, p1_r.at[r, side])
            go(first_far_copy, r, side)

        def block_on(r, ia):
            if ia == 3:
                all_in(block(r, 2, 0), p2_r.at[r])
            for side in range(2):
                go(second_copy, r, side, ia)
            to_core(r, ia, 0)

        def second_copy(r, side, ia):
            there = block(r, DELTAS[ia], 0)
            return copy(there if ia else own_block(r), there, q1_s.at[r], q1_r.at[r, side, ia], axis(r, 2)(ahead(side)))

        def second_far_copy(r, ia):
            side = ia // 2
            there = block(r, DELTAS[ia], back(side))
            return copy(there, there, q2_s.at[r], q2_r.at[r, ia], axis(r, 2)(ahead(side)))

        def second_forward(r, ia, side):
            there = block(r, DELTAS[ia], back(side))
            all_in(there, q1_r.at[r, side, ia])
            if ia // 2 == side:
                go(second_far_copy, r, ia)
            to_core(r, ia, 1 if side == 0 else 2)

        def second_far(r, ia):
            there = block(r, DELTAS[ia], 2)
            all_in(there, q2_r.at[r, ia])
            to_core(r, ia, 3)

        def some_rows(r, count):
            return rings[r][1].at[pl.ds(0, count * rows), rings[r][2]]

        def chunk_in(ia):
            all_in(some_rows(0, RING), cc_r.at[ia])

        def rows_in(r):
            all_in(some_rows(r, RING * RING), cc_r.at[RING - 1 + r])

        def own_wait(t):
            there = slot(t, 0, NEAR[0])
            pltpu.make_async_copy(there, there, own_sem.at[t]).wait()

        def own_rows(r):
            return pltpu.make_async_copy(own_block(r), block(r, 0, 0), own_sem.at[4 + r])

        def w_load(t):
            return pltpu.make_async_copy(fulls[t], (wv_a, held["wv_b"], wv_a, wv_r)[t], wv_sem.at[t])

        def row_load(src, i, buf):
            return pltpu.make_async_copy(src.at[chunk_rows(i)], rowbuf.at[buf], row_sem.at[buf])

        def chunk_loop(src, products, elementwise, between):
            row_load(src, 0, 0).start()
            between[0]()
            row_load(src, 1, 1).start()
            row_load(src, 0, 0).wait()
            products(0, 0)

            def body(i, carry):
                buf = lax.rem(i, 2)

                @pl.when(i + 1 < n_chunk)
                def _():
                    row_load(src, i + 1, 1 - buf).start()

                for k, step in enumerate(between[1:], 1):
                    pl.when(i == k)(step)
                row_load(src, i, buf).wait()
                free(elementwise, i - 1)
                elementwise(i - 1, 1 - buf, lambda: products(i, buf))
                return carry

            lax.fori_loop(1, n_chunk, body, 0)
            free(elementwise, n_chunk - 1)
            elementwise(n_chunk - 1, (n_chunk - 1) % 2, lambda: None)

        def free(elementwise, i):
            @pl.when(i >= 2)
            def _():
                for cp in copies_of[elementwise](i - 2):
                    cp.wait()

        def chunk_rows(i):
            return pl.ds(pl.multiple_of(i * chunk, chunk), chunk)

        def h_copies(i, which, names):
            xx, c = lax.div(i, 2), lax.rem(i, 2)
            cs = [pltpu.make_async_copy(hst.at[c, n], h_main.at[j, xx, c], hst_sem.at[c, n]) for n, j in enumerate(names)]
            return cs + [pltpu.make_async_copy(hst_rest.at[which, c], h_rest.at[which, xx, c], hst_sem.at[c, 2])]

        def keep(i, c, values):
            which = len(values) - 1
            for n, (j, v) in enumerate(values):
                low = v.astype(BF16)
                hst[c, n] = low[:, :main]
                hst_rest[which, c, :, j * rest:(j + 1) * rest] = low[:, main:]
                ff[j, :, chunk_rows(i)] = v.T.astype(BF16)

        def kept(elementwise):
            for i in (n_chunk - 2, n_chunk - 1):
                for cp in copies_of[elementwise](i):
                    cp.wait()

        def gate_work():
            def place(k):
                ia, flip = lax.div(k, 2), lax.rem(k, 2)
                delta = lax.rem(3 * ia + 3 * lax.div(ia, 2) + 2 * lax.div(ia, 3), RING)
                return 2 * lax.rem(x + delta, RING) + lax.rem(core + flip, 2)

            def body(k, carry):
                for n, group in enumerate(GATE_STEPS):
                    if group:
                        pl.when(k == n)(functools.partial(run, group))

                @pl.when(k < n_chunk)
                def _():
                    row_load(tok_all, place(k), lax.rem(k, 2)).start()

                @pl.when(k >= 1)
                def _():
                    i, buf = place(k - 1), lax.rem(k - 1, 2)
                    row_load(tok_all, i, buf).wait()
                    rb_ = rowbuf[buf]
                    av[chunk_rows(i), :main] = jnp.dot(rb_, wv_a[...], preferred_element_type=F32).astype(BF16)
                    both = jnp.dot(rb_, wv_r[...], preferred_element_type=F32).astype(BF16)
                    av[chunk_rows(i), main:] = both[:, :rest]
                    bv[chunk_rows(i), main:] = both[:, rest:2 * rest]

                return carry

            lax.fori_loop(0, n_chunk + 1, body, 0)

        def up_products(i, buf):
            bv[chunk_rows(i), :main] = jnp.dot(rowbuf[buf], held["wv_b"][...], preferred_element_type=F32).astype(BF16)

        def hidden(i, c, beside):
            a, b = av[chunk_rows(i)].astype(F32), bv[chunk_rows(i)].astype(F32)
            beside()
            keep(i, c, ((2, a * jax.nn.sigmoid(a) * b),))
            start(copies_of[hidden](i))

        def down_products(i, buf):
            rb_ = rowbuf[buf]
            lanes = 2 * rest // LANE * LANE
            low = jnp.dot(rb_, wv_r[:, lanes:], preferred_element_type=F32)[:, 2 * rest - lanes:3 * rest - lanes]
            gv[buf] = jnp.concatenate([jnp.dot(rb_, wv_a[...], preferred_element_type=F32), low], axis=1).astype(BF16)

        def backward(i, c, beside):
            g = gv[c].astype(F32)
            a, b = av[chunk_rows(i)].astype(F32), bv[chunk_rows(i)].astype(F32)
            beside()
            sig = jax.nn.sigmoid(a)
            keep(i, c, ((0, g * b * sig * (1.0 + a * (1.0 - sig))), (1, g * (a * sig))))
            start(copies_of[backward](i))

        copies_of = {hidden: lambda i: h_copies(i, 0, (2,)), backward: lambda i: h_copies(i, 1, (0, 1))}

        steps = (exchange, z_first, z_second, first_own, first_forward, block_on, second_forward, second_far, weights_done, chunk_in)

        def run(group):
            for which, *args in group:
                steps[which](*args)

        def rows_ready():
            run(UP_STEPS[-1])
            for r in (1, 2):
                own_rows(r).wait()
                rows_in(r)
            blk_load(plan[0][0], 0, plan[0][1]).start()

        def gather_phase(shard, pieces, rests, wv_b):
            held.update(shard=shard, pieces=pieces, rests=rests, wv_b=wv_b)
            with jax.named_scope("begin"):
                shard_load(0).start()
                shard_load(0).wait()
                for t in (1, 2):
                    shard_load(t).start()
                cut_pieces(0)
                pl.semaphore_wait(barrier, len(others))
                for r in range(3):
                    own_rows(r).start()
            with jax.named_scope("gather"):
                cut = {0}
                for step in GATHER_STEPS:
                    if step[0] in (EX, Z1) and step[1] not in cut:
                        if len(cut) == 1:
                            rests[...] = jnp.zeros_like(rests)
                            hst_rest[...] = jnp.zeros_like(hst_rest)
                            shard_load(1).wait()
                            shard_load(2).wait()
                        cut.add(step[1])
                        cut_pieces(step[1])
                    run((step,))
                own_rows(0).wait()
                w_load(0).wait()
                w_load(REST).wait()
            with jax.named_scope("gate"):
                gate_work()
            with jax.named_scope("up"):
                run(UP_STEPS[0])
                w_load(1).wait()
                chunk_loop(tok_all, up_products, hidden, [functools.partial(run, group) for group in ((),) + UP_STEPS[1:-1]] + [rows_ready])
                kept(hidden)
            for _, t in LATE_STEPS:
                own_wait(t)
            for t in range(4):
                all_out(some(t, n8 - 1), ex_s.at[t])
                all_out(some(t, 2 * n8), z1_s.at[t])

        pl.run_scoped(
            gather_phase, pltpu.VMEM((3,) + sg.shape, BF16), pltpu.VMEM((3, n8, dp, main), BF16), pltpu.VMEM((n8, dp, packed), BF16),
            pltpu.VMEM((d, main), BF16))
        run_order({
            "far_block": far_block, "next_products": next_products, "give_rows": give_rows, "late": functools.partial(run, LATE_STEPS),
        }, EARLY_ORDER)
        with jax.named_scope("down"):
            w_load(2).wait()
            chunk_loop(grad_all, down_products, backward, [lambda: None])
            kept(backward)
        for t in range(4):
            all_out(some(t, n8), z2_s.at[t])
        for r in range(3):
            for count, sem in ((2, p1_s), (1, p2_s), (2 * RING, q1_s), (RING, q2_s), (RING * RING, cc_s)):
                all_out(some_rows(r, count), sem.at[r])

    def backward_phase(tmp, stage):
        def next_adds(t):
            all_in(ra.at[t], a_r.at[t])
            cs = [pltpu.make_async_copy(ra.at[t, at], tmp.at[s, at], tmp_sem.at[s]) for s, at in ((0, lo), (1, hi))]
            start(cs)
            for c, (s, at) in zip(cs, ((0, lo), (1, hi))):
                c.wait()
                nxt[t, s, at] += tmp[s, at]
            for tile in range(tiles):
                start(c for s, c in enumerate(unit_copies(t, tile)) if (s, tile) not in early_units(t))

        def next_blocks(t):
            next_products(t)
            next_adds(t)

        def own_block(t):
            all_out(ra.at[t], a_s.at[t])
            product(t, far.at[t])

        def slot(t):
            return Z_ORDER.index(t) % 2

        def hand_out(t, tile, part):
            parts = unit_parts(t, tile)
            for k in reversed(range(n8)):
                dx, dc = NEAR[k]
                at = pl.ds(hand_at[dx][dc], dp)
                src, dst = stage.at[slot(t), tile, at], outs[t].at[i8, tile]

                def send(k=k, src=src, dst=dst):
                    if k:
                        rcopy(src, dst, e_s.at[t], e_r.at[t], near(*NEAR[k])).start()
                    else:
                        pltpu.make_async_copy(src, dst, out_sem.at[t]).start()

                if len(parts) == 1:
                    send()
                elif part == 0:
                    pl.when(xs[dx] < parts[0][2] // dp // 2)(send)
                else:
                    pl.when(xs[dx] >= parts[0][2] // dp // 2)(send)

        def handed(t):
            all_out(outs[t].at[pl.ds(0, n8 - 1)], e_s.at[t])
            pltpu.make_async_copy(outs[t].at[0], outs[t].at[0], out_sem.at[t]).wait()

        given = []

        def finish(t, tile):
            at = tile_rows(tile)
            wide = pl.ds(tile * LANE, LANE)
            for part, (n, first, size) in enumerate(unit_parts(t, tile)):
                lanes = pl.ds(first, size)
                all_in(rb.at[t, :, at, lanes], u_r.at[t, n])
                cs = [pltpu.make_async_copy(rb.at[t, s, at, lanes], tmp.at[s, at, lanes], tmp_sem.at[s]) for s in range(2)]
                start(cs)
                if t == Z_ORDER[2] and not given:
                    given.append(Z_ORDER[0])
                    handed(Z_ORDER[0])
                for c in cs:
                    c.wait()
                stage[slot(t), tile, lanes] = (far[t, wide, lanes] + tmp[0, wide, lanes] + tmp[1, wide, lanes]).T
                hand_out(t, tile, part)

        def on_y(r, n):
            return (r == 1) == (n == 1)

        def level(r, n):
            at = ys if on_y(r, n) else xs
            dev = ydev if on_y(r, n) else xdev
            if n == 1:
                def piece(k, h):
                    return part.at[r, pl.ds(2 * h, 2), at[k]] if on_y(r, n) else part.at[r, at[k], pl.ds(2 * h, 2)]
                return dev, piece, ra1, rb1, sd1, (a1_s, a1_r, f1_s, f1_r)

            def piece(k, h):
                return mid.at[r, at[k], pl.ds(h, 1)]
            return dev, piece, ra2, rb2, sd2, (a2_s, a2_r, f2_s, f2_r)

        def ring_a(r, n):
            dev, piece, rfar, _, _, sems = level(r, n)
            return [rcopy(piece(2, s), rfar.at[r, s], sems[0].at[r], sems[1].at[r], dev(1 + 2 * s)) for s in range(2)]

        def ring_f(r, n):
            dev, piece, _, rnear, _, sems = level(r, n)
            return [rcopy(piece(1 + 2 * s, 1 - s), rnear.at[r, s, 1 - s], sems[2].at[r], sems[3].at[r], dev(1 + 2 * s)) for s in range(2)]

        def ring_d(r, n):
            dev, _, _, rnear, dep, sems = level(r, n)
            return [rcopy(dep.at[r, s], rnear.at[r, s, s], sems[2].at[r], sems[3].at[r], dev(1 + 2 * s)) for s in range(2)]

        def add(grid, *terms):
            specs = []
            for ref, at, lead in terms:
                tail = ref.shape[lead:]
                specs.append(pl.BlockSpec((1,) * lead + tuple(tail), lambda *i, at=at, rank=len(tail): tuple(at(*i)) + (0,) * rank))

            def body(*refs):
                total = refs[0][...].astype(F32).reshape(refs[0].shape[-2:])
                for ref in refs[1:-1]:
                    total = total + ref[...].astype(F32).reshape(total.shape)
                refs[-1][...] = total.astype(BF16).reshape(refs[-1].shape)

            pltpu.emit_pipeline(body, grid=grid, in_specs=specs[:-1], out_specs=specs[-1:])(*[ref for ref, _, _ in terms])

        def ring_first(r, n):
            start(ring_a(r, n) + ring_f(r, n))

        def ring_dependent(r, n):
            _, _, rfar, _, _, sems = level(r, n)
            all_in(rfar.at[r], sems[1].at[r])
            here = y if on_y(r, n) else x
            if n == 1:
                def near_block(s, i):
                    at = lax.rem(here + 1 + 2 * s, RING)
                    return (2 * s + i, at) if on_y(r, n) else (at, 2 * s + i)

                add((2, 2), (part.at[r], near_block, 2), (ra1.at[r], lambda s, i: (s, i), 2), (sd1.at[r], lambda s, i: (s, i), 2))
            else:
                add((2,), (mid.at[r], lambda s: (lax.rem(here + 1 + 2 * s, RING), s), 2), (ra2.at[r], lambda s: (s, 0), 2),
                    (sd2.at[r], lambda s: (s, 0), 2))
            start(ring_d(r, n))

        def ring_last(r, n):
            _, _, _, rnear, _, sems = level(r, n)
            all_in(rnear.at[r], sems[3].at[r])
            here = y if on_y(r, n) else x
            if n == 1:
                def own_at(h, i):
                    return (2 * h + i, here) if on_y(r, n) else (here, 2 * h + i)

                add((2, 2), (part.at[r], own_at, 2), (rb1.at[r, 0], lambda h, i: (h, i), 2),
                    (rb1.at[r, 1], lambda h, i: (h, i), 2), (mid.at[r], lambda h, i: (2 * h + i,), 1))
            else:
                own, res = ((tok_own, out), (grad_own, gin))[r]
                add((2,), (own, lambda h: (h,), 1), (mid.at[r], lambda h: (here, h), 2), (rb2.at[r, 0], lambda h: (h, 0), 2),
                    (rb2.at[r, 1], lambda h: (h, 0), 2), (res, lambda h: (h,), 1))

        def keep_rows(r):
            core_copy(r).wait_recv()
            row_products(r, True)

        run_order({
            "far_block": far_block, "next_products": next_products, "next_adds": next_adds, "next_blocks": next_blocks,
            "own_block": own_block, "finish": finish, "give_rows": give_rows, "keep_rows": keep_rows, "ring_first": ring_first,
            "ring_dependent": ring_dependent, "ring_last": ring_last,
        }, LATE_ORDER)

        for t in range(3):
            all_out(nxt.at[t], u_s.at[t])
        for r in range(2):
            core_copy(r).wait_send()
            for n in (1, 2):
                _, _, rfar, rnear, _, sems = level(r, n)
                all_out(rfar.at[r], sems[0].at[r])
                all_out(rnear.at[r], sems[2].at[r])
        for t in Z_ORDER:
            with jax.named_scope(f"handed_{t}"):
                all_in(outs[t].at[pl.ds(0, n8 - 1)], e_r.at[t])
                if t not in given:
                    handed(t)

    pl.run_scoped(
        forward_phase,
        pltpu.VMEM((2, chunk, d), BF16),
        pltpu.VMEM((tokens, nf), BF16),
        pltpu.VMEM((tokens, nf), BF16),
        pltpu.VMEM((2, chunk, nf), BF16),
        pltpu.VMEM((2, 2, chunk, main), BF16),
        pltpu.VMEM((2, 2, chunk, packed), BF16),
        pltpu.VMEM((d, main), BF16),
        pltpu.VMEM((d, packed), BF16),
    )
    pl.run_scoped(backward_phase, pltpu.VMEM((2, tiles * LANE, cols), F32), pltpu.VMEM((2, tiles, cols, LANE), F32))


def layer(sg, su, sd, tok, grad):
    n8 = 2 * RING
    dp, nf = sg.shape[0], sg.shape[1] // n8
    rows, d = tok.shape
    tokens = rows * RING * n8
    cols = d // RING
    tiles = -(-nf // LANE)
    padded = tiles * LANE
    main = nf // LANE * LANE
    packed = -(-3 * (nf - main) // LANE) * LANE
    hbm = pl.BlockSpec(memory_space=pl.ANY)
    dma = pltpu.SemaphoreType.DMA
    sds = jax.ShapeDtypeStruct
    halves = (2, rows // 2, d)
    res = pl.pallas_call(
        layer_kernel,
        out_shape=[sds((n8, tiles, dp, LANE), F32)] * 3 + [sds(halves, BF16)] * 2 + [
            sds((d, main), BF16), sds((d, main), BF16), sds((d, main), BF16), sds((d, packed), BF16), sds((tokens, d), BF16), sds((tokens, d), BF16),
            sds((3, RING, 2, RING * rows, main), BF16), sds((2, RING, 2, RING * rows, packed), BF16),
            sds((3, nf, cols), F32), sds((3, 2, nf, cols), F32),
            sds((2, RING, RING, rows, d), BF16), sds((2, RING, RING, rows, d), BF16), sds((2, RING, RING, rows, d), BF16),
            sds((2, 2, 2, rows, d), BF16), sds((2, 2, 2, 2, rows, d), BF16), sds((2, 2, 2, rows, d), BF16),
            sds((2, RING, 2, rows // 2, d), BF16),
            sds((2, 2, 1, rows // 2, d), BF16), sds((2, 2, 2, 1, rows // 2, d), BF16), sds((2, 2, 1, rows // 2, d), BF16),
        ],
        in_specs=[hbm] * 7,
        out_specs=[hbm] * 25,
        scratch_shapes=[
            pltpu.VMEM((3, nf, tokens), BF16),
            pltpu.VMEM((2, tokens, cols), BF16),
            pltpu.VMEM((3, padded, cols), F32),
            pltpu.VMEM((3, 2, nf, cols), F32),
            dma((7,)),
            dma((4,)), dma((4, n8)),
            dma((4,)), dma((4, 2, n8 // 2)), dma((4,)),
            dma((4,)),
            dma((3,)), dma((3, 2)),
            dma((3,)), dma((3,)),
            dma((3,)), dma((3, 2, RING)),
            dma((3,)), dma((3, RING)),
            dma((3,)), dma((RING + 2,)),
            dma((3,)), dma((4,)), dma((2,)), dma((2, 3)), dma((2,)), dma((2,)),
            dma((3,)), dma((3,)),
            dma((3,)), dma((3, tiles + 1)),
            dma((3,)), dma((3,)),
            dma((3,)),
            dma((2,)), dma((2,)),
        ] + [dma((2,))] * 8,
        compiler_params=pltpu.CompilerParams(collective_id=0, has_side_effects=True, vmem_limit_bytes=67043328),
        cost_estimate=pl.CostEstimate(flops=18 * nf * tokens * d, bytes_accessed=300_000_000, transcendentals=0),
        name="layer",
    )(sg, su, sd, tok, grad, tok.reshape(halves), grad.reshape(halves))
    return res[:3], res[3].reshape(rows, d), res[4].reshape(rows, d)


def assemble_kernel(og, ou, od, out, gin, g, u, w, res, gres, buf, flat, in_sem, out_sem, row_buf, row_sem):
    n8, nf = og.shape[0], g.shape[1] // og.shape[0]
    srcs, dsts = (og, ou, od), (g, u, w)
    rows_in = [pltpu.make_async_copy(src, row_buf.at[r], row_sem.at[r]) for r, src in enumerate((out, gin))]
    loads = [pltpu.make_async_copy(src, buf.at[t], in_sem.at[t]) for t, src in enumerate(srcs)]
    stores = [pltpu.make_async_copy(flat.at[t], dst, out_sem.at[t]) for t, dst in enumerate(dsts)]
    for c in loads + rows_in:
        c.start()
    for t in range(3):
        loads[t].wait()
        for j in range(n8):
            flat[t, :, j * nf:(j + 1) * nf] = jnp.concatenate([buf[t, j, tile] for tile in range(buf.shape[2])], axis=1)[:, :nf]
        stores[t].start()
    rows_out = [pltpu.make_async_copy(row_buf.at[r], dst, row_sem.at[r]) for r, dst in enumerate((res, gres))]
    for c in rows_in:
        c.wait()
    for c in rows_out:
        c.start()
    for c in stores + rows_out:
        c.wait()


def assemble(sums, out, gin, ff):
    dp = sums[0].shape[2]
    hbm = pl.BlockSpec(memory_space=pl.ANY)
    dma = pltpu.SemaphoreType.DMA
    sds = jax.ShapeDtypeStruct
    return pl.pallas_call(
        assemble_kernel,
        out_shape=[sds((dp, ff), F32)] * 3 + [sds(out.shape, BF16)] * 2,
        in_specs=[hbm] * 5,
        out_specs=[hbm] * 5,
        scratch_shapes=[
            pltpu.VMEM((3,) + sums[0].shape, F32), pltpu.VMEM((3, dp, ff), F32), dma((3,)), dma((3,)),
            pltpu.VMEM((2,) + out.shape, BF16), dma((2,)),
        ],
        compiler_params=pltpu.CompilerParams(vmem_limit_bytes=63 * 1024 * 1024),
        name="assemble",
    )(*sums, out, gin)


def solution(mesh):
    nz, ny, nd = mesh.shape["datb"], mesh.shape["model"], mesh.shape["data"]
    fine = Mesh(mesh.devices.reshape(nz, ny, nd // 2, 2), ("datb", "model", "x", "core"))

    def local_step(tok_loc, wg_loc, wu_loc, wd_loc, grad_loc):
        sums, out, grad_in = layer(wg_loc, wu_loc, wd_loc.T, tok_loc, grad_loc)
        grad_gate, grad_up, grad_down_t, out, grad_in = assemble(sums, out, grad_in, wg_loc.shape[1])
        return out, grad_in, grad_gate, grad_up, grad_down_t.T

    return jax.shard_map(local_step, mesh=fine, in_specs=(ROW_SPEC, GATE_SPEC, GATE_SPEC, DOWN_SPEC, ROW_SPEC), out_specs=(ROW_SPEC, ROW_SPEC, GATE_SPEC, GATE_SPEC, DOWN_SPEC), check_vma=False)
```

profile of v0, /device:TPU:1, one launch (start us, length us, event | category | flops | bytes accessed | tf_op | source)
XLA Modules:
  0.0 333.3 jit_solution(6633306912255201261)
XLA Ops:
  0.6 327.1 %layer.1 = (f32[8,5,112,128]{3,2,1,0:T(8,128)}, f32[8,5,112,128]{3,2,1,0:T(8,128)}, f32[8,5,112,128]{3,2,1,0:T(8,128)}, bf16[2,32,3584]{2,1,0:T(8,128)(2,1)}, bf...) custom-call(bf16[112,4736]{1,0:T(8,128)(2,1)} %sg.1, ...), custom_call_target="tpu_custom_call" | custom-call | flops 78215380992 | bytes 300000000 | tf_op jit(solution)/shard_map/layer/pallas_call | solution.py:826
  327.7 5.4 %assemble.1 = (f32[112,4736]{1,0:T(8,128)}, f32[112,4736]{1,0:T(8,128)}, f32[112,4736]{1,0:T(8,128)}, bf16[64,3584]{1,0:T(8,128)(2,1)}, bf16[64,3584]{1,0:T(8,128)(2,1)}) custom-call(f32[8,5,112,128]{3,2,1,0:T(8,128)} %get-tuple-element.15.og, f32[8,5,112,128]{3,2,1,0:T(8,128)} %get-tuple-element.16.ou, f32[8,5,112,128]{3,2,1,0:T(8,128)} %get-tuple-element.17.od, ...), custom_call_target="tpu_custom_call" | custom-call | tf_op jit(solution)/shard_map/assemble/pallas_call | solution.py:894
where the time goes:
time: 336 us; the launch traced here: 333 us
  Pallas kernels  332 us (99%)
    pallas_call x1, Pallas kernels, layer(): pl.pallas_call(layer_kernel, out_shape=[sds((n8, tiles, dp, LANE), F32)]...  327 us

commit v1 on v0

--- a/solution.py
+++ b/solution.py
@@ -868,13 +868,18 @@
     n8, nf = og.shape[0], g.shape[1] // og.shape[0]
     srcs, dsts = (og, ou, od), (g, u, w)
     rows_in = [pltpu.make_async_copy(src, row_buf.at[r], row_sem.at[r]) for r, src in enumerate((out, gin))]
-    loads = [pltpu.make_async_copy(src, buf.at[t], in_sem.at[t]) for t, src in enumerate(srcs)]
+    some = n8 // 2
+    loads = [
+        pltpu.make_async_copy(src.at[pl.ds(h * some, some)], buf.at[t, pl.ds(h * some, some)], in_sem.at[2 * t + h])
+        for t, src in enumerate(srcs) for h in range(2)
+    ]
     stores = [pltpu.make_async_copy(flat.at[t], dst, out_sem.at[t]) for t, dst in enumerate(dsts)]
     for c in loads + rows_in:
         c.start()
     for t in range(3):
-        loads[t].wait()
         for j in range(n8):
+            if j % some == 0:
+                loads[2 * t + j // some].wait()
             flat[t, :, j * nf:(j + 1) * nf] = jnp.concatenate([buf[t, j, tile] for tile in range(buf.shape[2])], axis=1)[:, :nf]
         stores[t].start()
     rows_out = [pltpu.make_async_copy(row_buf.at[r], dst, row_sem.at[r]) for r, dst in enumerate((res, gres))]
@@ -897,7 +902,7 @@
         in_specs=[hbm] * 5,
         out_specs=[hbm] * 5,
         scratch_shapes=[
-            pltpu.VMEM((3,) + sums[0].shape, F32), pltpu.VMEM((3, dp, ff), F32), dma((3,)), dma((3,)),
+            pltpu.VMEM((3,) + sums[0].shape, F32), pltpu.VMEM((3, dp, ff), F32), dma((6,)), dma((3,)),
             pltpu.VMEM((2,) + out.shape, BF16), dma((2,)),
         ],
         compiler_params=pltpu.CompilerParams(vmem_limit_bytes=63 * 1024 * 1024),

time: 336 us -> 336 us (level)
  no operation moved by 1% of the time
where the time goes in v1:
time: 336 us; the launch traced here: 334 us
  Pallas kernels  333 us (99%)
    pallas_call x1, Pallas kernels, layer(): pl.pallas_call(layer_kernel, out_shape=[sds((n8, tiles, dp, LANE), F32)]...  327 us

profile of v1, /device:TPU:1, one launch (start us, length us, event | category | flops | bytes accessed | tf_op | source)
XLA Modules:
  0.0 333.5 jit_solution(4588916707011765052)
XLA Ops:
  0.6 327.1 %layer.1 = (f32[8,5,112,128]{3,2,1,0:T(8,128)}, f32[8,5,112,128]{3,2,1,0:T(8,128)}, f32[8,5,112,128]{3,2,1,0:T(8,128)}, bf16[2,32,3584]{2,1,0:T(8,128)(2,1)}, bf...) custom-call(bf16[112,4736]{1,0:T(8,128)(2,1)} %sg.1, ...), custom_call_target="tpu_custom_call" | custom-call | flops 78215380992 | bytes 300000000 | tf_op jit(solution)/shard_map/layer/pallas_call | solution.py:826
  327.7 5.6 %assemble.1 = (f32[112,4736]{1,0:T(8,128)}, f32[112,4736]{1,0:T(8,128)}, f32[112,4736]{1,0:T(8,128)}, bf16[64,3584]{1,0:T(8,128)(2,1)}, bf16[64,3584]{1,0:T(8,128)(2,1)}) custom-call(f32[8,5,112,128]{3,2,1,0:T(8,128)} %get-tuple-element.15.og, f32[8,5,112,128]{3,2,1,0:T(8,128)} %get-tuple-element.16.ou, f32[8,5,112,128]{3,2,1,0:T(8,128)} %get-tuple-element.17.od, ...), custom_call_target="tpu_custom_call" | custom-call | tf_op jit(solution)/shard_map/assemble/pallas_call | solution.py:899
